TPU v7x, 512 devices: a whole 4x8x8 slice. The times are simulated.
512 devices in a mesh: row: 32 (over z, y_lo, core), col: 16 (over x, y_hi).
Axes of the slice: x: 4, y: 8 (y_hi: 4, y_lo: 2; y = y_hi * 2 + y_lo), z: 8, core: 2. Of those that a mesh axis runs over, the one named last changes fastest.
Arguments:
- pair_exchange: bfloat16 [1024, 16, 1024], P(('row', 'col')), may hold values from -6 to 6
- conduction: bfloat16 [1024, 4, 1024], P(('row', 'col')), may hold values from -6 to 6
- valence: bfloat16 [1024, 4, 1024], P(('row', 'col')), may hold values from -6 to 6
- coulomb: float32 [1024], replicated, may hold values from 0.5 to 5
- screening: float32 [289, 1024], replicated, may hold values from 0.1 to 1
- energies: float32 [1024, 16], P(('row', 'col')), may hold values from 1 to 9
- vectors: bfloat16 [1024, 512], P(('row', 'col')), may hold values from -6 to 6
- k_coords: int32 [1024, 2], P(('row', 'col')), may hold values from 0 to 31, as said below
Outputs:
- residual_block: float32 [1024, 512], P(('row', 'col'))
- alpha: float32 [32, 32], replicated
Inputs may be any that keep to these rules, and one draw needn't show every extreme that they name: `k_coords`: each row holds a k-point's coordinates on the periodic 32 x 32 mesh, first then second; every mesh point occurs exactly once.
All inputs are finite; a program needn't handle non-finite values.
Results may differ from a plain program's by a relative error of at most 0.0028.
Values may be sent and summed in bfloat16 or wider, within the bound.
No kernel may reach another device: no remote copies, remote signals or barrier semaphores. Data moves between devices by JAX's collectives and lax.ppermute only.
A program may use at most 64 MiB of HBM per device.

v0:
```python
import functools
import jax
import jax.numpy as jnp
from jax import lax
from jax.sharding import Mesh
from jax.sharding import PartitionSpec as P

MX = 32
ROW = ("row_0", "row_1", "row_2")
COL = ("col_0", "col_1")
ROW_COL = ("row_0", "row_1", "row_2", "col_0", "col_1")
highest = lax.Precision.HIGHEST


def over_axes(x, axes):
    return functools.reduce(lax.psum, axes, x)


def pair_factors(conduction, valence):
    count, valence_count, plane_count = valence.shape
    joined = (
        valence.astype(jnp.float32)[:, :, None, :] * conduction.astype(jnp.float32)[:, None, :, :]
    )
    return joined.reshape(count, valence_count * conduction.shape[1], plane_count).astype(
        jnp.bfloat16
    )


def transfer_index(rows_at, cols_at, mesh_cols):
    delta_first = jnp.mod(rows_at[:, None, 0] - cols_at[None, :, 0], MX)
    delta_second = jnp.mod(rows_at[:, None, 1] - cols_at[None, :, 1], mesh_cols)
    fold_first = jnp.minimum(delta_first, MX - delta_first)
    fold_second = jnp.minimum(delta_second, mesh_cols - delta_second)
    return (fold_first * (mesh_cols // 2 + 1) + fold_second).astype(jnp.int32)


def on_device(pair_exchange, conduction, valence, coulomb, screening, energies, vectors, k_coords):
    local_count, band_count, plane_count = pair_exchange.shape
    vector_count = vectors.shape[1] // band_count
    row_count = lax.axis_size(ROW)
    col_count = lax.axis_size(COL)
    total_count = local_count * row_count * col_count
    mesh_cols = total_count // MX
    moving = vectors.reshape(local_count, band_count, vector_count)
    partial_density = jnp.einsum(
        "ktg,ktn->gn", pair_exchange, moving, preferred_element_type=jnp.float32
    )
    density = lax.psum(partial_density, ROW_COL)
    block_size = 128
    sweeps = plane_count // block_size
    col_cond, col_val, col_vec, col_at = (
        lax.all_gather(conduction, ROW, axis=0, tiled=True),
        lax.all_gather(valence, ROW, axis=0, tiled=True),
        lax.all_gather(vectors, ROW, axis=0, tiled=True),
        lax.all_gather(k_coords, ROW, axis=0, tiled=True),
    )
    row_cond, row_val, row_at = (
        lax.all_gather(conduction, COL, axis=0, tiled=True),
        lax.all_gather(valence, COL, axis=0, tiled=True),
        lax.all_gather(k_coords, COL, axis=0, tiled=True),
    )
    row_pairs = pair_factors(row_cond, row_val)
    col_pairs = pair_factors(col_cond, col_val)
    indices = transfer_index(row_at, col_at, mesh_cols)
    col_moving = col_vec.reshape(-1, band_count, vector_count)

    def square_sweep(sweep_index, running):
        anchor = sweep_index * block_size
        coupling = jnp.take(
            lax.dynamic_slice_in_dim(screening, anchor, block_size, 1), indices, axis=0
        )
        row_block = lax.dynamic_slice_in_dim(row_pairs, anchor, block_size, 2)
        col_block = lax.dynamic_slice_in_dim(col_pairs, anchor, block_size, 2)
        col_proj = jnp.einsum(
            "ktg,ktn->kng", col_block, col_moving, preferred_element_type=jnp.float32
        )
        potential = jnp.einsum("ijg,jng->ing", coupling, col_proj, precision=highest)
        return running + jnp.einsum(
            "ktg,kng->ktn", row_block.astype(jnp.float32), potential, precision=highest
        )

    forward = lax.fori_loop(
        0,
        sweeps,
        square_sweep,
        jnp.zeros((row_pairs.shape[0], band_count, vector_count), jnp.float32),
    )
    owned = lax.psum_scatter(
        forward.reshape(col_count, local_count, band_count, vector_count),
        COL,
        scatter_dimension=0,
        tiled=True,
    )[0]
    moving_wide = moving.astype(jnp.float32)
    exchange_term = jnp.einsum(
        "ktg,gn->ktn", pair_exchange.astype(jnp.float32) * coulomb, density, precision=highest
    )
    applied = (
        energies[:, :, None] * moving_wide
        + 2.0 / (total_count * band_count) * exchange_term
        - owned / total_count
    )
    gram = jnp.einsum("ktm,ktn->mn", moving_wide, applied, precision=highest)
    alpha = over_axes(gram, ROW_COL) / (total_count * band_count)
    residual = applied - jnp.einsum("ktm,mn->ktn", moving_wide, alpha, precision=highest)
    return (residual.reshape(local_count, band_count * vector_count), alpha)


def solution(mesh):
    split = Mesh(mesh.devices.reshape(8, 2, 2, 4, 4), ("row_0", "row_1", "row_2", "col_0", "col_1"))
    return jax.shard_map(
        on_device,
        mesh=split,
        in_specs=(
            P(ROW_COL, None, None),
            P(ROW_COL, None, None),
            P(ROW_COL, None, None),
            P(),
            P(),
            P(ROW_COL, None),
            P(ROW_COL, None),
            P(ROW_COL, None),
        ),
        out_specs=(P(ROW_COL, None), P()),
        check_vma=False,
    )
```

profile of v0, /device:TPU:8, one launch (start us, length us, event | category | flops | bytes accessed | tf_op | source)
XLA Modules:
  0.0 629.1 jit_solution(7728930901200443616)
XLA Ops:
  8.8 1.7 convolution_bitcast_fusion.1
  10.6 37.5 %all-gather.2 = s32[32,2,2]{2,1,0:T(2,128)S(1)} all-gather(s32[1,2,2]{2,1,0:T(2,128)} %bitcast.67), channel_id=1, replica_groups=mesh['row_0'=8,'row_1'=2,'row_2'=2,'col_0'=4,'col_1'=4] {'row_0','row_1'..., dimensions={0}, use_global_device_ids=true | all-gather | bytes 528 | tf_op jit(solution)/shard_map/all_gather | solution.py:55
  48.1 44.7 %all-gather.1 = s32[16,2,2]{2,1,0:T(2,128)S(1)} all-gather(s32[1,2,2]{2,1,0:T(2,128)} %bitcast.68), channel_id=1, replica_groups=mesh['row_0'=8,'row_1'=2,'row_2'=2,'col_0'=4,'col_1'=4] {'col_0','col_1'}, dimensions={0}, use_global_device_ids=true | all-gather | bytes 272 | tf_op jit(solution)/shard_map/all_gather | solution.py:60
  92.8 35.3 %all_gather.23 = bf16[64,4,1024]{2,1,0:T(4,128)(2,1)S(1)} all-gather(bf16[2,4,1024]{2,1,0:T(4,128)(2,1)} %param.12), channel_id=1, replica_groups=mesh['row_0'=8,'row_1'=2,'row_2'=2,'col_0'=4,'col_1'=4] {'row_0','row_1'..., dimensions={0}, use_global_device_ids=true | all-gather | bytes 540672 | tf_op jit(solution)/shard_map/all_gather | solution.py:53
  128.1 39.7 %all_gather.21 = bf16[32,4,1024]{2,1,0:T(4,128)(2,1)S(1)} all-gather(bf16[2,4,1024]{2,1,0:T(4,128)(2,1)} %param.12), channel_id=1, replica_groups=mesh['row_0'=8,'row_1'=2,'row_2'=2,'col_0'=4,'col_1'=4] {'col_0','col_1'}, dimensions={0}, use_global_device_ids=true | all-gather | bytes 278528 | tf_op jit(solution)/shard_map/all_gather | solution.py:59
  167.8 32.9 %all_gather.24 = bf16[64,4,1024]{2,1,0:T(4,128)(2,1)S(1)} all-gather(bf16[2,4,1024]{2,1,0:T(4,128)(2,1)} %param.11), channel_id=1, replica_groups=mesh['row_0'=8,'row_1'=2,'row_2'=2,'col_0'=4,'col_1'=4] {'row_0','row_1'..., dimensions={0}, use_global_device_ids=true | all-gather | bytes 540672 | tf_op jit(solution)/shard_map/all_gather | solution.py:52
  200.7 42.9 %all_gather.22 = bf16[32,4,1024]{2,1,0:T(4,128)(2,1)S(1)} all-gather(bf16[2,4,1024]{2,1,0:T(4,128)(2,1)} %param.11), channel_id=1, replica_groups=mesh['row_0'=8,'row_1'=2,'row_2'=2,'col_0'=4,'col_1'=4] {'col_0','col_1'}, dimensions={0}, use_global_device_ids=true | all-gather | bytes 278528 | tf_op jit(solution)/shard_map/all_gather | solution.py:58
  244.3 1.5 multiply_convert_fusion
  245.8 2.1 convert_element_type.42
  249.8 32.5 %all-gather = bf16[32,2,512]{2,1,0:T(2,128)(2,1)S(1)} all-gather(bf16[1,2,512]{2,1,0:T(2,128)(2,1)S(1)} %bitcast.66), channel_id=1, replica_groups=mesh['row_0'=8,'row_1'=2,'row_2'=2,'col_0'=4,'col_1'=4] {'row_0','row_1'..., dimensions={0}, use_global_device_ids=true | all-gather | bytes 67584 | tf_op jit(solution)/shard_map/all_gather | solution.py:54
  282.5 178.4 %while.14 = (s32[]{:T(128)}, f32[32,16,32]{2,1,0:T(8,128)S(1)}, bf16[32,16,1024]{2,1,0:T(8,128)(2,1)}, bf16[64,16,1024]{2,1,0:T(8,128)(2,1)}, bf16[64,16,32]{2,1...) while((s32[]{:T(128)}, f32[32,16,32]{2,1,0:T(8,128)S(1)}, ...), condition=%wide.region_2.3_spmd.clone, body=%wide.region_1.2_spmd.clone.sunk | while | flops 134656000 | bytes 12475081 | solution.py:82
  283.6 5.5 gather_fusion
  289.1 2.8 copy.37
  293.2 2.9 copy.36
  296.2 5.7 fusion.49
  301.9 1.4 copy.38
  303.4 1.4 convolution_add_fusion.2
  305.9 5.5 gather_fusion
  311.4 2.8 copy.37
  315.5 2.9 copy.36
  318.5 5.7 fusion.49
  325.7 1.4 convolution_add_fusion.2
  328.2 5.5 gather_fusion
  333.7 2.8 copy.37
  337.8 2.9 copy.36
  340.8 5.7 fusion.49
  346.5 1.4 copy.38
  348.0 1.4 convolution_add_fusion.2
  350.5 5.5 gather_fusion
  356.0 2.8 copy.37
  360.1 2.9 copy.36
  363.1 5.7 fusion.49
  368.8 1.4 copy.38
  370.3 1.4 convolution_add_fusion.2
  372.8 5.5 gather_fusion
  378.3 2.8 copy.37
  382.4 2.9 copy.36
  385.4 5.7 fusion.49
  391.1 1.4 copy.38
  392.6 1.4 convolution_add_fusion.2
  395.1 5.5 gather_fusion
  400.6 2.8 copy.37
  404.7 2.9 copy.36
  407.7 5.7 fusion.49
  413.4 1.4 copy.38
  414.9 1.4 convolution_add_fusion.2
  417.4 5.5 gather_fusion
  422.9 2.8 copy.37
  427.0 2.9 copy.36
  430.0 5.7 fusion.49
  435.7 1.4 copy.38
  437.2 1.4 convolution_add_fusion.2
  439.7 5.5 gather_fusion
  445.2 2.8 copy.37
  449.3 2.9 copy.36
  452.3 5.7 fusion.49
  458.0 1.4 copy.38
  459.5 1.4 convolution_add_fusion.2
  461.6 80.6 %reduce-scatter.2.cloned.1.call-done = f32[1,2,16,32]{3,2,1,0:T(8,128)} async-done(((f32[16,2,16,32]{3,2,1,0:T(8,128)}), f32[1,2,16,32]{3,2,1,0:T(8,128)}) %reduce-scatter.2.cloned.1.call-update) | async-done | bytes 4112 | tf_op jit(solution)/shard_map/reduce_scatter | solution.py:88
  543.6 30.9 %psum.43 = f32[32,32]{0,1:T(8,128)S(1)} all-reduce(f32[32,32]{0,1:T(8,128)S(1)} %convolution_bitcast_fusion.3), channel_id=1, replica_groups=mesh['row_0'=8,'row_1'=2,'row_2'=2,'col_0'=4,'col_1'=4] {'row_0'}, use_global_device_ids=true, to_apply=%region_4.5 | all-reduce | flops 1024 | bytes 8192 | tf_op jit(solution)/shard_map/psum | solution.py:16
  574.5 8.1 %psum.44 = f32[32,32]{0,1:T(8,128)S(1)} all-reduce(f32[32,32]{0,1:T(8,128)S(1)} %psum.43), channel_id=1, replica_groups=mesh['row_0'=8,'row_1'=2,'row_2'=2,'col_0'=4,'col_1'=4] {'row_1'}, use_global_device_ids=true, to_apply=%region_5.6 | all-reduce | flops 1024 | bytes 8192 | tf_op jit(solution)/shard_map/psum | solution.py:16
  582.6 3.3 psum.45
  586.0 15.9 %psum.46 = f32[32,32]{0,1:T(8,128)S(1)} all-reduce(f32[32,32]{0,1:T(8,128)S(1)} %psum.45), channel_id=1, replica_groups=mesh['row_0'=8,'row_1'=2,'row_2'=2,'col_0'=4,'col_1'=4] {'col_0'}, use_global_device_ids=true, to_apply=%region_7.8 | all-reduce | flops 1024 | bytes 8192 | tf_op jit(solution)/shard_map/psum | solution.py:16
  601.9 18.3 %psum.47 = f32[32,32]{0,1:T(8,128)S(1)} all-reduce(f32[32,32]{0,1:T(8,128)S(1)} %psum.46), channel_id=1, replica_groups=mesh['row_0'=8,'row_1'=2,'row_2'=2,'col_0'=4,'col_1'=4] {'col_1'}, use_global_device_ids=true, to_apply=%region_8.9 | all-reduce | flops 1024 | bytes 8192 | tf_op jit(solution)/shard_map/psum | solution.py:16
  (85 shorter events, 28.6 us)
Async XLA Ops:
  8.0 453.6 %all-reduce.2.cloned.1.call-start = ((), (), s32[]{:S(2)}) async-start(), calls=%async_computation.1 | async-start | bytes 262144 | tf_op jit(solution)/shard_map/psum | solution.py:48
  10.5 531.8 %reduce-scatter.2.cloned.1.call-start = ((), (), s32[]{:S(2)}) async-start(), calls=%async_computation.2 | async-start | bytes 278528 | tf_op jit(solution)/shard_map/reduce_scatter | solution.py:88
  248.0 1.7 copy-start.2
  282.5 259.8 %copy-start.1 = (bf16[2,16,1024]{2,1,0:T(8,128)(2,1)S(1)}, bf16[2,16,1024]{2,1,0:T(8,128)(2,1)}, u32[]{:S(2)}) copy-start(bf16[2,16,1024]{2,1,0:T(8,128)(2,1)} %param.10) | copy-start | bytes 196612
  282.5 259.8 %copy-start.3 = (f32[1024]{0:T(1024)S(1)}, f32[1024]{0:T(1024)}, u32[]{:S(2)}) copy-start(f32[1024]{0:T(1024)} %param.13) | copy-start | bytes 12292
  282.5 259.8 %copy-start.4 = (f32[2,16]{1,0:T(2,128)S(1)}, f32[2,16]{1,0:T(2,128)}, u32[]{:S(2)}) copy-start(f32[2,16]{1,0:T(2,128)} %param.15) | copy-start | bytes 388
  460.9 0.7 copy-start
Sparse Core Ops, SparseCore 0:
  13.8 270.8 all-reduce.1
Sparse Core Ops, SparseCore 1:
  461.7 80.5 reduce-scatter.1
where the time goes:
time: 630 us; the launch traced here: 629 us
  blocking collectives  342 us (54%)
  local copies, waits for them, and re-layouts  115 us (18%)
  waiting for transfers between devices  80.7 us (13%)
  matrix products  70.7 us (11%)
  between operations  15.6 us (2%)
    reduce_scatter x1, waiting for transfers between devices, on_device(): lax.psum_scatter(forward.reshape(col_count, local_count, band_count, vect...  80.6 us
    psum x5, blocking collectives, over_axes(): return functools.reduce(lax.psum, axes, x)  76.5 us
    gather x16, local copies, waits for them, and re-layouts, square_sweep(): jnp.take(lax.dynamic_slice_in_dim(screening, anchor, block_size, 1), indi...  66.3 us
    dot_general x8, matrix products, square_sweep(): jnp.einsum('ijg,jng->ing', coupling, col_proj, precision=highest)  45.6 us
    all_gather x1, blocking collectives, on_device(): lax.all_gather(k_coords, COL, axis=0, tiled=True)  44.7 us
    all_gather x1, blocking collectives, on_device(): lax.all_gather(conduction, COL, axis=0, tiled=True)  42.9 us
    all_gather x1, blocking collectives, on_device(): lax.all_gather(valence, COL, axis=0, tiled=True)  39.7 us
    all_gather x1, blocking collectives, on_device(): lax.all_gather(k_coords, ROW, axis=0, tiled=True)  37.5 us
  transfers between devices with their start and end apart: 2, of which 1 were waited for; matrix products, arithmetic and copies ran while one was open for 29% of the time, Pallas kernels for 0%

commit v1 on v0

--- a/solution.py
+++ b/solution.py
@@ -54,10 +54,13 @@
         lax.all_gather(vectors, ROW, axis=0, tiled=True),
         lax.all_gather(k_coords, ROW, axis=0, tiled=True),
     )
+    lead_strings = lambda across, dim_at, vals: jnp.concatenate(
+        lax.all_to_all(jnp.stack([vals] * lax.axis_size(across)), across, 0, 0), dim_at
+    )
     row_cond, row_val, row_at = (
         lax.all_gather(conduction, COL, axis=0, tiled=True),
         lax.all_gather(valence, COL, axis=0, tiled=True),
-        lax.all_gather(k_coords, COL, axis=0, tiled=True),
+        lead_strings(COL, 0, k_coords),
     )
     row_pairs = pair_factors(row_cond, row_val)
     col_pairs = pair_factors(col_cond, col_val)

time: 630 us -> 603 us (0.957)
  blocking collectives: 342 us -> 301 us
  starting transfers between devices: 0.08 us -> 8.9 us
    all_gather x1 -> x0, blocking collectives: 44.7 us -> none  [on_device(): lax.all_gather(k_coords, COL, axis=0, tiled=True)]
    all_to_all x0 -> x1, starting transfers between devices: none -> 8.82 us  [on_device(): lax.all_to_all(jnp.stack([vals] * lax.axis_size(across)), across, 0, 0)]
    all_gather x1, blocking collectives: 37.5 us -> 31 us  [on_device(): lax.all_gather(k_coords, ROW, axis=0, tiled=True)]
  transfers between devices with their start and end apart: 2 -> 3, of which waited for: 1 -> 1; matrix products, arithmetic and copies ran while one was open for 29% -> 31% of each run, Pallas kernels for 0% -> 0%
where the time goes in v1:
time: 603 us; the launch traced here: 602 us
  blocking collectives  301 us (50%)
  local copies, waits for them, and re-layouts  118 us (20%)
  waiting for transfers between devices  83.1 us (14%)
  matrix products  70.7 us (12%)
  between operations  15.6 us (3%)
  starting transfers between devices  8.9 us (1%)
    reduce_scatter x1, waiting for transfers between devices, on_device(): lax.psum_scatter(forward.reshape(col_count, local_count, band_count, vect...  83 us
    psum x5, blocking collectives, over_axes(): return functools.reduce(lax.psum, axes, x)  76.5 us
    gather x16, local copies, waits for them, and re-layouts, square_sweep(): jnp.take(lax.dynamic_slice_in_dim(screening, anchor, block_size, 1), indi...  66.3 us
    all_gather x1, blocking collectives, on_device(): lax.all_gather(valence, COL, axis=0, tiled=True)  45.9 us
    dot_general x8, matrix products, square_sweep(): jnp.einsum('ijg,jng->ing', coupling, col_proj, precision=highest)  45.6 us
    all_gather x1, blocking collectives, on_device(): lax.all_gather(valence, ROW, axis=0, tiled=True)  40.2 us
    all_gather x1, blocking collectives, on_device(): lax.all_gather(conduction, COL, axis=0, tiled=True)  39.6 us
    all_gather x1, blocking collectives, on_device(): lax.all_gather(conduction, ROW, axis=0, tiled=True)  35.2 us
  transfers between devices with their start and end apart: 3, of which 1 were waited for; matrix products, arithmetic and copies ran while one was open for 31% of the time, Pallas kernels for 0%

profile of v1, /device:TPU:8, one launch (start us, length us, event | category | flops | bytes accessed | tf_op | source)
XLA Modules:
  0.0 601.8 jit_solution(224860272760985447)
XLA Ops:
  9.4 8.8 %all-to-all-start = ((s32[16,2,2]{1,2,0:T(2,128)}), s32[16,2,2]{1,2,0:T(2,128)}, u32[]{:S(2)}, u32[]{:S(2)}) async-start(s32[16,2,2]{1,2,0:T(2,128)} %stack.2), calls=%async_computation | async-start | bytes 32768 | tf_op jit(solution)/shard_map/all_to_all | solution.py:58
  19.0 1.7 convolution_bitcast_fusion.1
  20.8 40.2 %all_gather.20 = bf16[64,4,1024]{2,1,0:T(4,128)(2,1)S(1)} all-gather(bf16[2,4,1024]{2,1,0:T(4,128)(2,1)} %param.12), channel_id=1, replica_groups=mesh['row_0'=8,'row_1'=2,'row_2'=2,'col_0'=4,'col_1'=4] {'row_0','row_1'..., dimensions={0}, use_global_device_ids=true | all-gather | bytes 540672 | tf_op jit(solution)/shard_map/all_gather | solution.py:53
  61.0 45.9 %all_gather.18 = bf16[32,4,1024]{2,1,0:T(4,128)(2,1)S(1)} all-gather(bf16[2,4,1024]{2,1,0:T(4,128)(2,1)} %param.12), channel_id=1, replica_groups=mesh['row_0'=8,'row_1'=2,'row_2'=2,'col_0'=4,'col_1'=4] {'col_0','col_1'}, dimensions={0}, use_global_device_ids=true | all-gather | bytes 278528 | tf_op jit(solution)/shard_map/all_gather | solution.py:62
  107.0 35.2 %all_gather.21 = bf16[64,4,1024]{2,1,0:T(4,128)(2,1)S(1)} all-gather(bf16[2,4,1024]{2,1,0:T(4,128)(2,1)} %param.11), channel_id=1, replica_groups=mesh['row_0'=8,'row_1'=2,'row_2'=2,'col_0'=4,'col_1'=4] {'row_0','row_1'..., dimensions={0}, use_global_device_ids=true | all-gather | bytes 540672 | tf_op jit(solution)/shard_map/all_gather | solution.py:52
  142.2 39.6 %all_gather.19 = bf16[32,4,1024]{2,1,0:T(4,128)(2,1)S(1)} all-gather(bf16[2,4,1024]{2,1,0:T(4,128)(2,1)} %param.11), channel_id=1, replica_groups=mesh['row_0'=8,'row_1'=2,'row_2'=2,'col_0'=4,'col_1'=4] {'col_0','col_1'}, dimensions={0}, use_global_device_ids=true | all-gather | bytes 278528 | tf_op jit(solution)/shard_map/all_gather | solution.py:61
  181.8 31.0 %all-gather.1 = s32[32,2,2]{2,1,0:T(2,128)S(1)} all-gather(s32[1,2,2]{2,1,0:T(2,128)} %bitcast.67), channel_id=1, replica_groups=mesh['row_0'=8,'row_1'=2,'row_2'=2,'col_0'=4,'col_1'=4] {'row_0','row_1'..., dimensions={0}, use_global_device_ids=true | all-gather | bytes 528 | tf_op jit(solution)/shard_map/all_gather | solution.py:55
  213.6 32.7 %all-gather = bf16[32,2,512]{2,1,0:T(2,128)(2,1)S(1)} all-gather(bf16[1,2,512]{2,1,0:T(2,128)(2,1)S(1)} %bitcast.66), channel_id=1, replica_groups=mesh['row_0'=8,'row_1'=2,'row_2'=2,'col_0'=4,'col_1'=4] {'row_0','row_1'..., dimensions={0}, use_global_device_ids=true | all-gather | bytes 67584 | tf_op jit(solution)/shard_map/all_gather | solution.py:54
  246.3 1.5 multiply_convert_fusion
  248.6 2.1 convert_element_type.42
  252.8 178.4 %while.14 = (s32[]{:T(128)}, f32[32,16,32]{2,1,0:T(8,128)S(1)}, bf16[32,16,1024]{2,1,0:T(8,128)(2,1)}, bf16[64,16,1024]{2,1,0:T(8,128)(2,1)}, bf16[64,16,32]{2,1...) while((s32[]{:T(128)}, f32[32,16,32]{2,1,0:T(8,128)S(1)}, ...), condition=%wide.region_2.3_spmd.clone, body=%wide.region_1.2_spmd.clone.sunk | while | flops 134656000 | bytes 12475081 | solution.py:85
  254.0 5.5 gather_fusion
  259.4 2.8 copy.35
  263.6 2.9 copy.34
  266.6 5.7 fusion.48
  272.3 1.4 copy.36
  273.7 1.4 convolution_add_fusion.2
  276.3 5.5 gather_fusion
  281.7 2.8 copy.35
  285.9 2.9 copy.34
  288.9 5.7 fusion.48
  294.6 1.4 copy.36
  296.0 1.4 convolution_add_fusion.2
  298.6 5.5 gather_fusion
  304.0 2.8 copy.35
  308.2 2.9 copy.34
  311.2 5.7 fusion.48
  316.9 1.4 copy.36
  318.3 1.4 convolution_add_fusion.2
  320.9 5.5 gather_fusion
  326.4 2.8 copy.35
  330.5 2.9 copy.34
  333.5 5.7 fusion.48
  339.2 1.4 copy.36
  340.6 1.4 convolution_add_fusion.2
  343.2 5.5 gather_fusion
  348.6 2.8 copy.35
  352.8 2.9 copy.34
  355.8 5.7 fusion.48
  361.5 1.4 copy.36
  362.9 1.4 convolution_add_fusion.2
  365.5 5.5 gather_fusion
  370.9 2.8 copy.35
  375.1 2.9 copy.34
  378.1 5.7 fusion.48
  383.8 1.4 copy.36
  385.2 1.4 convolution_add_fusion.2
  387.8 5.5 gather_fusion
  393.2 2.8 copy.35
  397.4 2.9 copy.34
  400.4 5.7 fusion.48
  406.1 1.4 copy.36
  407.5 1.4 convolution_add_fusion.2
  410.1 5.5 gather_fusion
  415.5 2.8 copy.35
  419.7 2.9 copy.34
  422.7 5.7 fusion.48
  429.8 1.4 convolution_add_fusion.2
  432.0 83.0 %reduce-scatter.2.cloned.1.call-done = f32[1,2,16,32]{3,2,1,0:T(8,128)} async-done(((f32[16,2,16,32]{3,2,1,0:T(8,128)}), f32[1,2,16,32]{3,2,1,0:T(8,128)}) %reduce-scatter.2.cloned.1.call-update) | async-done | bytes 4112 | tf_op jit(solution)/shard_map/reduce_scatter | solution.py:91
  516.4 30.8 %psum.43 = f32[32,32]{0,1:T(8,128)S(1)} all-reduce(f32[32,32]{0,1:T(8,128)S(1)} %convolution_bitcast_fusion.3), channel_id=1, replica_groups=mesh['row_0'=8,'row_1'=2,'row_2'=2,'col_0'=4,'col_1'=4] {'row_0'}, use_global_device_ids=true, to_apply=%region_4.5 | all-reduce | flops 1024 | bytes 8192 | tf_op jit(solution)/shard_map/psum | solution.py:16
  547.2 8.1 %psum.44 = f32[32,32]{0,1:T(8,128)S(1)} all-reduce(f32[32,32]{0,1:T(8,128)S(1)} %psum.43), channel_id=1, replica_groups=mesh['row_0'=8,'row_1'=2,'row_2'=2,'col_0'=4,'col_1'=4] {'row_1'}, use_global_device_ids=true, to_apply=%region_5.6 | all-reduce | flops 1024 | bytes 8192 | tf_op jit(solution)/shard_map/psum | solution.py:16
  555.3 3.3 psum.45
  558.6 15.9 %psum.46 = f32[32,32]{0,1:T(8,128)S(1)} all-reduce(f32[32,32]{0,1:T(8,128)S(1)} %psum.45), channel_id=1, replica_groups=mesh['row_0'=8,'row_1'=2,'row_2'=2,'col_0'=4,'col_1'=4] {'col_0'}, use_global_device_ids=true, to_apply=%region_7.8 | all-reduce | flops 1024 | bytes 8192 | tf_op jit(solution)/shard_map/psum | solution.py:16
  574.6 18.3 %psum.47 = f32[32,32]{0,1:T(8,128)S(1)} all-reduce(f32[32,32]{0,1:T(8,128)S(1)} %psum.46), channel_id=1, replica_groups=mesh['row_0'=8,'row_1'=2,'row_2'=2,'col_0'=4,'col_1'=4] {'col_1'}, use_global_device_ids=true, to_apply=%region_8.9 | all-reduce | flops 1024 | bytes 8192 | tf_op jit(solution)/shard_map/psum | solution.py:16
  (88 shorter events, 30.8 us)
Async XLA Ops:
  9.4 242.6 %all-to-all-start = ((s32[16,2,2]{1,2,0:T(2,128)}), s32[16,2,2]{1,2,0:T(2,128)}, u32[]{:S(2)}, u32[]{:S(2)}) async-start(s32[16,2,2]{1,2,0:T(2,128)} %stack.2), calls=%async_computation | async-start | bytes 32768 | tf_op jit(solution)/shard_map/all_to_all | solution.py:58
  18.2 413.8 %all-reduce.2.cloned.1.call-start = ((), (), s32[]{:S(2)}) async-start(), calls=%async_computation.2 | async-start | bytes 262144 | tf_op jit(solution)/shard_map/psum | solution.py:48
  20.7 494.3 %reduce-scatter.2.cloned.1.call-start = ((), (), s32[]{:S(2)}) async-start(), calls=%async_computation.3 | async-start | bytes 278528 | tf_op jit(solution)/shard_map/reduce_scatter | solution.py:91
  212.9 0.7 copy-start.2
  252.8 262.2 %copy-start.1 = (bf16[2,16,1024]{2,1,0:T(8,128)(2,1)S(1)}, bf16[2,16,1024]{2,1,0:T(8,128)(2,1)}, u32[]{:S(2)}) copy-start(bf16[2,16,1024]{2,1,0:T(8,128)(2,1)} %param.10) | copy-start | bytes 196612
  252.8 262.2 %copy-start.3 = (f32[1024]{0:T(1024)S(1)}, f32[1024]{0:T(1024)}, u32[]{:S(2)}) copy-start(f32[1024]{0:T(1024)} %param.13) | copy-start | bytes 12292
  252.8 262.2 %copy-start.4 = (f32[2,16]{1,0:T(2,128)S(1)}, f32[2,16]{1,0:T(2,128)}, u32[]{:S(2)}) copy-start(f32[2,16]{1,0:T(2,128)} %param.15) | copy-start | bytes 388
  431.3 0.7 copy-start
Sparse Core Ops, SparseCore 0:
  24.0 271.7 all-reduce.1
Sparse Core Ops, SparseCore 1:
  432.1 82.9 reduce-scatter.1
